TPU v7x, 32 devices: a whole 2x2x4 slice. The times are simulated.
32 devices in a mesh: gx: 4 (over y, core), gy: 4 (over z), gz: 2 (over x).
Axes of the slice: x: 2, y: 2, z: 4, core: 2. Of those that a mesh axis runs over, the one named last changes fastest.
Arguments:
- residual: float32 [32, 128, 256], P('gx', 'gy', 'gz'), may hold values from -32 to 32
- direction: float32 [32, 128, 256], P('gx', 'gy', 'gz'), may hold values from -32 to 32
- diagonal: float32 [32, 128, 256], P('gx', 'gy', 'gz'), may hold values from 0.5 to 2
- recycled: bfloat16 [16, 32, 128, 256], P(None, 'gx', 'gy', 'gz'), may hold values from -6 to 6
- recycled_images: bfloat16 [16, 32, 128, 256], P(None, 'gx', 'gy', 'gz'), may hold values from -0.0014648438 to 0.0014648438
- coupling_inverse: float32 [16, 16], replicated, may hold values from -1 to 3, as said below
Outputs:
- solution_delta: float32 [32, 128, 256], P('gx', 'gy', 'gz')
- new_residual: float32 [32, 128, 256], P('gx', 'gy', 'gz')
- new_direction: float32 [32, 128, 256], P('gx', 'gy', 'gz')
Inputs may be any that keep to these rules, and one draw needn't show every extreme that they name: `coupling_inverse`: symmetric.
All inputs are finite; a program needn't handle non-finite values.
Results may differ from a plain program's by a relative error of at most 0.0028.
Values sent between devices are 32-bit elements; how exact they have to be, the bound alone decides.
No kernel may reach another device: no remote copies, remote signals or barrier semaphores. Data moves between devices by JAX's collectives and lax.ppermute only.
A program may use at most 64 MiB of HBM per device.

v0:
```python
import jax
import jax.numpy as jnp
import numpy as np
from jax import lax
from jax.sharding import PartitionSpec as P

S = 4
BASIS = 9
center = 7.25
half_width = 6.75


def extended(block, sides, width):
    for axis, dim in sides:
        count = lax.axis_size(axis)
        forward = [(i, i + 1) for i in range(count - 1)]
        forward.append((count - 1, 0))
        backward = [(target, source) for source, target in forward]
        low = lax.ppermute(
            lax.slice_in_dim(block, block.shape[dim] - width, None, axis=dim), axis, forward
        )
        high = lax.ppermute(lax.slice_in_dim(block, 0, width, axis=dim), axis, backward)
        block = jnp.concatenate([low, block, high], axis=dim)
    return block


def inside(padded):
    centre_cells = padded[:, 1:-1, 1:-1, 1:-1]
    beside_all = padded[:, 2:, 1:-1, 1:-1] + padded[:, :-2, 1:-1, 1:-1]
    beside_all = beside_all + padded[:, 1:-1, 2:, 1:-1] + padded[:, 1:-1, :-2, 1:-1]
    beside_all = beside_all + padded[:, 1:-1, 1:-1, 2:] + padded[:, 1:-1, 1:-1, :-2]
    return (centre_cells, beside_all)


def trim_margin(values, margin):
    if margin == 0:
        return values
    return values[..., margin:-margin, margin:-margin, margin:-margin]


def chebyshev_next(current, beside_all, diagonal, earlier):
    mapped = (6.0 + diagonal) * current - beside_all
    scaled = (mapped - center * current) / half_width
    if earlier is None:
        return scaled
    return 2.0 * scaled - earlier


def recurrence_matrix():
    recurrence = np.zeros((BASIS, BASIS), np.float32)
    for offset, length in ((0, S + 1), (S + 1, S)):
        recurrence[offset, offset] = center
        recurrence[offset + 1, offset] = half_width
        for column in range(1, length - 1):
            recurrence[offset + column + 1, offset + column] = half_width / 2
            recurrence[offset + column, offset + column] = center
            recurrence[offset + column - 1, offset + column] = half_width / 2
    return jnp.asarray(recurrence, dtype=jnp.float32)


def coordinates(totals, coupling_inverse):
    precise = lax.Precision.HIGHEST
    gram_block = totals[:BASIS]
    projections = totals[BASIS:]
    recurrence = recurrence_matrix()
    counter = jnp.arange(BASIS)
    residue = (counter == S + 1).astype(jnp.float32)
    search = (counter == 0).astype(jnp.float32)
    update = jnp.zeros((BASIS,), jnp.float32)
    norm_now = jnp.dot(residue, jnp.dot(gram_block, residue, precision=precise), precision=precise)
    for iteration in range(S):
        mapped = jnp.dot(recurrence, search, precision=precise)
        step_size = norm_now / jnp.dot(
            search, jnp.dot(gram_block, mapped, precision=precise), precision=precise
        )
        update = update + step_size * search
        residue = residue - step_size * mapped
        norm_next = jnp.dot(
            residue, jnp.dot(gram_block, residue, precision=precise), precision=precise
        )
        search = residue + norm_next / norm_now * search
        norm_now = norm_next
    weights = jnp.dot(
        coupling_inverse, jnp.dot(projections, residue, precision=precise), precision=precise
    )
    return (update, residue, search, weights.astype(jnp.bfloat16))


def body(residual, direction, diagonal, recycled, recycled_images, coupling_inverse):
    precise = lax.Precision.HIGHEST
    search_basis = [direction]
    residue_basis = [residual]
    earlier = None
    packed = jnp.stack([direction, residual, diagonal])
    padded = extended(packed, (("gx", 1), ("gy", 2), ("gz", 3)), S)
    wide_diag = padded[2]
    current = padded[:2]
    for iteration in range(S):
        if iteration == S - 1:
            current = current[:1]
            earlier = earlier[:1]
        centre_cells, beside_all = inside(current)
        margin = S - iteration - 1
        local_diag = trim_margin(wide_diag, iteration + 1)
        previous = None if earlier is None else trim_margin(earlier, 2)
        following = chebyshev_next(centre_cells, beside_all, local_diag, previous)
        earlier, current = (current, following)
        search_basis.append(trim_margin(following[0], margin))
        if following.shape[0] > 1:
            residue_basis.append(trim_margin(following[1], margin))
    basis = jnp.stack(search_basis + residue_basis)
    basis_flat = basis.reshape(basis.shape[0], -1)
    gram_block = lax.dot_general(
        basis_flat,
        basis_flat,
        (((1,), (1,)), ((), ())),
        precision=precise,
        preferred_element_type=jnp.float32,
    )
    rounded = basis_flat.astype(jnp.bfloat16)
    images = recycled_images.reshape(recycled_images.shape[0], -1)
    projections = lax.dot_general(
        images, rounded, (((1,), (1,)), ((), ())), preferred_element_type=jnp.float32
    )
    totals = lax.psum(jnp.concatenate([gram_block, projections], 0), ("gx", "gy", "gz"))
    update, residue, search, weights = coordinates(totals, coupling_inverse)
    shape = residual.shape
    solution_delta = jnp.dot(update, basis_flat, precision=precise).reshape(shape)
    new_residual = jnp.dot(residue, basis_flat, precision=precise).reshape(shape)
    correction = jnp.dot(
        weights, recycled.reshape(recycled.shape[0], -1), preferred_element_type=jnp.float32
    )
    new_direction = (jnp.dot(search, basis_flat, precision=precise) - correction).reshape(shape)
    return (solution_delta, new_residual, new_direction)


def solution(mesh):
    in_specs = (
        P("gx", "gy", "gz"),
        P("gx", "gy", "gz"),
        P("gx", "gy", "gz"),
        P(None, "gx", "gy", "gz"),
        P(None, "gx", "gy", "gz"),
        P(),
    )
    out_specs = (P("gx", "gy", "gz"), P("gx", "gy", "gz"), P("gx", "gy", "gz"))
    return jax.shard_map(body, mesh=mesh, in_specs=in_specs, out_specs=out_specs, check_vma=False)
```

profile of v0, /device:TPU:0, one launch (start us, length us, event | category | flops | bytes accessed | tf_op | source)
XLA Modules:
  0.0 110.9 jit_solution(13209403578807758797)
XLA Ops:
  0.7 1.1 %pad_maximum_fusion.2 = f32[3,8,32,128]{3,2,1,0:T(8,128)S(1)} fusion(f32[1,8,32,128]{3,2,1,0:T(8,128)} %bitcast.257, f32[1,8,32,128]{3,2,1,0:T(8,128)} %bitcast.251, f32[1,8,32,128]{3,2,1,0:T(8,128)} %bitcast.245), kind=kLoop, calls=%fused_computation.81 | loop fusion | flops 196608 | bytes 786432 | tf_op jit(solution)/shard_map/stack | solution.py:94
  1.8 0.5 collective-permute-start
  2.4 2.0 %collective-permute-start.1 = (f32[3,4,32,128]{3,2,1,0:T(8,128)S(1)}, f32[3,4,32,128]{3,2,1,0:T(8,128)S(1)}, u32[]{:S(2)}, u32[]{:S(2)}) collective-permute-start(f32[3,4,32,128]{3,2,1,0:T(8,128)S(1)} %get-tuple-element.14), channel_id=1, source_target_pairs={{8,0},{16,8},{24,16},{0,24},{9,1},{17,9},{25,17},{1,25},{10,2},{18... | collective-permute-start | bytes 589832 | tf_op jit(solution)/shard_map/ppermute | solution.py:22
  4.4 3.3 %collective-permute-done = f32[3,4,32,128]{3,2,1,0:T(8,128)S(1)} collective-permute-done((f32[3,4,32,128]{3,2,1,0:T(8,128)S(1)}, f32[3,4,32,128]{3,2,1,0:T(8,128)S(1)}, u32[]{:S(2)}, u32[]{:S(2)}) %collective-permute-start) | collective-permute-done | bytes 196640 | tf_op jit(solution)/shard_map/ppermute | solution.py:19
  7.7 1.9 %collective-permute-done.1 = f32[3,4,32,128]{3,2,1,0:T(8,128)S(1)} collective-permute-done((f32[3,4,32,128]{3,2,1,0:T(8,128)S(1)}, f32[3,4,32,128]{3,2,1,0:T(8,128)S(1)}, u32[]{:S(2)}, u32[]{:S(2)}) %collective-permute-start.1) | collective-permute-done | bytes 196640 | tf_op jit(solution)/shard_map/ppermute | solution.py:22
  9.6 0.9 pad_maximum_fusion.7
  10.5 1.6 %collective-permute-start.2 = (f32[3,16,4,128]{3,2,1,0:T(4,128)S(1)}, f32[3,16,4,128]{3,2,1,0:T(4,128)S(1)}, u32[]{:S(2)}, u32[]{:S(2)}) collective-permute-start(f32[3,16,4,128]{3,2,1,0:T(4,128)S(1)} %get-tuple-element.11), channel_id=1, source_target_pairs={{0,2},{2,4},{4,6},{6,0},{1,3},{3,5},{5,7},{7,1},{8,10},{10,12},{12... | collective-permute-start | bytes 294920 | tf_op jit(solution)/shard_map/ppermute | solution.py:19
  12.1 2.2 %collective-permute-start.3 = (f32[3,16,4,128]{3,2,1,0:T(4,128)S(1)}, f32[3,16,4,128]{3,2,1,0:T(4,128)S(1)}, u32[]{:S(2)}, u32[]{:S(2)}) collective-permute-start(f32[3,16,4,128]{3,2,1,0:T(4,128)S(1)} %get-tuple-element.12), channel_id=1, source_target_pairs={{2,0},{4,2},{6,4},{0,6},{3,1},{5,3},{7,5},{1,7},{10,8},{12,10},{14... | collective-permute-start | bytes 294920 | tf_op jit(solution)/shard_map/ppermute | solution.py:22
  14.4 3.7 %collective-permute-done.2 = f32[3,16,4,128]{3,2,1,0:T(4,128)S(1)} collective-permute-done((f32[3,16,4,128]{3,2,1,0:T(4,128)S(1)}, f32[3,16,4,128]{3,2,1,0:T(4,128)S(1)}, u32[]{:S(2)}, u32[]{:S(2)}) %collective-permute-start.2) | collective-permute-done | bytes 98336 | tf_op jit(solution)/shard_map/ppermute | solution.py:19
  18.0 1.4 %collective-permute-done.3 = f32[3,16,4,128]{3,2,1,0:T(4,128)S(1)} collective-permute-done((f32[3,16,4,128]{3,2,1,0:T(4,128)S(1)}, f32[3,16,4,128]{3,2,1,0:T(4,128)S(1)}, u32[]{:S(2)}, u32[]{:S(2)}) %collective-permute-start.3) | collective-permute-done | bytes 98336 | tf_op jit(solution)/shard_map/ppermute | solution.py:22
  19.4 0.1 pad_maximum_fusion.1
  19.6 0.3 fusion.105
  19.9 0.4 copy.18
  20.3 1.6 %collective-permute-start.4 = (f32[3,16,40,4]{2,1,3,0:T(8,128)S(1)}, f32[3,16,40,4]{2,1,3,0:T(8,128)S(1)}, u32[]{:S(2)}, u32[]{:S(2)}) collective-permute-start(f32[3,16,40,4]{2,1,3,0:T(8,128)S(1)} %copy.18), channel_id=1, source_target_pairs={{0,1},{1,0},{2,3},{3,2},{4,5},{5,4},{6,7},{7,6},{8,9},{9,8},{10,11... | collective-permute-start | bytes 92168 | tf_op jit(solution)/shard_map/ppermute | solution.py:19
  21.8 0.4 copy.19
  22.2 0.6 collective-permute-start.5
  22.8 0.1 fusion.55
  22.9 2.8 %collective-permute-done.4 = f32[3,16,40,4]{2,1,3,0:T(8,128)S(1)} collective-permute-done((f32[3,16,40,4]{2,1,3,0:T(8,128)S(1)}, f32[3,16,40,4]{2,1,3,0:T(8,128)S(1)}, u32[]{:S(2)}, u32[]{:S(2)}) %collective-permute-start.4) | collective-permute-done | bytes 30752 | tf_op jit(solution)/shard_map/ppermute | solution.py:19
  25.7 0.4 copy.20
  26.1 1.0 collective-permute-done.5
  27.1 0.4 copy.21
  27.5 1.1 pad_maximum_fusion
  28.6 0.2 slice_add_fusion.15
  28.8 0.2 slice_add_fusion.16
  29.0 0.2 slice_add_fusion.17
  29.2 1.9 %fusion.6 = f32[2,14,38,134]{3,2,1,0:T(8,128)S(1)} fusion(f32[3,16,40,136]{3,2,1,0:T(8,128)S(1)} %pad_maximum_fusion, f32[14,38,134]{2,1,0:T(8,128)S(1)} %slice_add_fusion.15), kind=kLoop, calls=%fused_computation.8 | loop fusion | flops 1425760 | bytes 4847584 | tf_op jit(solution)/shard_map/div | solution.py:43
  31.1 1.9 %slice_subtract_fusion = f32[2,12,36,132]{3,2,1,0:T(8,128)S(1)} fusion(f32[3,16,40,136]{3,2,1,0:T(8,128)S(1)} %pad_maximum_fusion, f32[2,14,38,134]{3,2,1,0:T(8,128)S(1)} %fusion.6, f32[12,36,132]{2,1,0:T(8,128)S(1)} %slice_add_fusion.16), kind=kLoop, calls=%fused_computation.43 | loop fusion | flops 1254528 | bytes 4333824 | tf_op jit(solution)/shard_map/sub | solution.py:46
  33.0 1.6 %slice_subtract_fusion.1 = f32[2,10,34,130]{3,2,1,0:T(8,128)S(1)} fusion(f32[2,14,38,134]{3,2,1,0:T(8,128)S(1)} %fusion.6, f32[2,12,36,132]{3,2,1,0:T(8,128)S(1)} %slice_subtract_fusion, f32[10,34,130]{2,1,0:T(8,128)S(1)} %slice_add_fusion.17), kind=kLoop, calls=%fused_computation.53 | loop fusion | flops 972400 | bytes 3359200 | tf_op jit(solution)/shard_map/sub | solution.py:46
  34.6 0.3 slice_subtract_fusion.2
  35.0 0.1 slice_bitcast_fusion.3
  35.1 0.1 slice_bitcast_fusion.1
  35.1 0.1 slice.279
  35.3 0.1 slice.294
  35.4 0.1 slice.268
  35.5 0.1 slice.292
  35.6 0.1 slice.290
  35.7 0.1 slice.257
  35.8 2.1 %stack.65 = f32[9,8,32,128]{3,0,2,1:T(8,128)S(1)} concatenate(f32[1,8,32,128]{3,0,2,1:T(1,128)S(1)} %bitcast.249, f32[1,8,32,128]{3,0,2,1:T(1,128)S(1)} %bitcast.273, f32[1,8,32,128]{3,0,2,1:T(1,128)S(1)} %bitcast.267, f32[1,8,32,128]{3,0,2,1:T(1,128)S(1)} %bitcast.263, f32[1,8,32,128]{3,0,2,1:T(1,128)S(1)} %bitcast.261, f32[1,8,32,128]{3,0,2,1:T(1,128)S(1)} %bitcast.255, ...), dimensions={0} | concatenate | bytes 2359296 | tf_op jit(solution)/shard_map/stack | solution.py:111
  37.8 2.9 %convolution_bitcast_fusion.1 = f32[9,9]{0,1:T(8,128)S(1)} fusion(f32[9,8,32,128]{3,0,2,1:T(8,128)S(1)} %stack.65), kind=kOutput, calls=%fused_computation.14 | convolution fusion | flops 31850496 | bytes 1179972 | tf_op jit(solution)/shard_map/dot_general | solution.py:113
  40.7 1.9 %stack.75 = f32[9,32768]{1,0:T(8,128)S(1)} concatenate(f32[1,32768]{1,0:T(1,128)S(1)} %bitcast.250, f32[1,32768]{1,0:T(1,128)S(1)} %bitcast.274, f32[1,32768]{1,0:T(1,128)S(1)} %bitcast.268, f32[1,32768]{1,0:T(1,128)S(1)} %bitcast.264, f32[1,32768]{1,0:T(1,128)S(1)} %bitcast.262, f32[1,32768]{1,0:T(1,128)S(1)} %bitcast.256, f32[1,32768]{1,0:T(1,128)S(1)} %bitcast.272, ...), dimensions={0} | concatenate | bytes 2359296 | tf_op jit(solution)/shard_map/stack | solution.py:111
  42.6 2.0 %convolution_bitcast_fusion = f32[16,9]{0,1:T(8,128)S(1)} fusion(bf16[2,8,256,128]{3,2,1,0:T(8,128)(2,1)} %bitcast.275, f32[9,32768]{1,0:T(8,128)S(1)} %stack.75), kind=kOutput, calls=%fused_computation.13 | convolution fusion | flops 9732096 | bytes 2228800 | tf_op jit(solution)/shard_map/dot_general | solution.py:122
  44.6 0.1 pad_maximum_fusion.8
  44.7 40.0 %psum.7 = f32[25,9]{0,1:T(8,128)S(1)} all-reduce(f32[25,9]{0,1:T(8,128)S(1)} %pad_maximum_fusion.8), channel_id=1, replica_groups=mesh['gx'=4,'gy'=4,'gz'=2] {'gx','gy','gz'}, use_global_device_ids=true, to_apply=%region_0.0 | all-reduce | flops 225 | bytes 1800 | tf_op jit(solution)/shard_map/psum | solution.py:125
  84.7 0.7 fusion.31
  85.4 0.7 fusion.30
  87.5 0.7 fusion.32
  89.6 0.1 fusion.89
  89.7 0.8 fusion.33
  91.8 0.7 fusion.34
  93.9 0.1 fusion.87
  94.0 0.8 fusion.35
  96.1 0.8 fusion.36
  98.3 0.1 fusion.85
  98.5 0.8 fusion.37
  100.6 0.2 convolution_bitcast_fusion.3
  100.8 0.7 fusion.38
  101.6 0.4 copy.55
  102.0 0.1 slice.297
  102.1 2.4 %fusion = f32[1,8,32,128]{3,0,2,1:T(1,128)} fusion(f32[8,32,128,9]{2,1,0,3:T(8,128)S(1)} %bitcast.242, f32[9]{0:T(128)S(1)} %fusion.67), kind=kOutput, calls=%fused_computation | convolution fusion | flops 3538944 | bytes 1310756 | tf_op jit(solution)/shard_map/dot_general | solution.py:129
  104.5 2.4 %fusion.2 = f32[1,8,32,128]{3,0,2,1:T(1,128)} fusion(f32[8,32,128,9]{2,1,0,3:T(8,128)S(1)} %bitcast.243, f32[9]{0:T(128)S(1)} %multiply_add_fusion, f32[9]{0:T(128)S(1)} %multiply_add_fusion.1, f32[9]{0:T(128)S(1)} %select_add_fusion, f32[]{:T(128)S(6)} %div.44, f32[]{:T(128)S(6)} %div.42, f32[]{:T(128)S(6)} %div.40, f32[]{:T(128)S(6)} %div.38), kind=kOutput, calls=%fused_computation.2 | convolution fusion | flops 3539016 | bytes 1310844 | tf_op jit(solution)/shard_map/dot_general | solution.py:128
  108.3 1.1 %fusion.62 = f32[1,32768]{1,0:T(1,128)S(1)} fusion(f32[9,32768]{1,0:T(8,128)S(1)} %stack.75, f32[9]{0:T(128)S(1)} %fusion.67, f32[9]{0:T(128)S(1)} %multiply_add_fusion, f32[]{:T(128)S(6)} %div.45), kind=kOutput, calls=%fused_computation.119 | convolution fusion | flops 3538962 | bytes 1310796 | tf_op jit(solution)/shard_map/dot_general | solution.py:133
  109.4 0.1 fusion.15
  109.5 0.7 fusion.18
  110.2 0.7 sub.63
  (21 shorter events, 0.2 us)
Async XLA Ops:
  0.6 108.8 %copy-start = (f32[16,16]{1,0:T(8,128)S(1)}, f32[16,16]{1,0:T(8,128)}, u32[]{:S(2)}) copy-start(f32[16,16]{1,0:T(8,128)} %param.12) | copy-start | bytes 3076
  0.6 18.8 %copy-start.1 = (f32[8,32,128]{2,1,0:T(8,128)S(1)}, f32[8,32,128]{2,1,0:T(8,128)}, u32[]{:S(2)}) copy-start(f32[8,32,128]{2,1,0:T(8,128)} %param.8) | copy-start | bytes 393220
  0.7 18.8 %copy-start.2 = (f32[8,32,128]{2,1,0:T(8,128)S(1)}, f32[8,32,128]{2,1,0:T(8,128)}, u32[]{:S(2)}) copy-start(f32[8,32,128]{2,1,0:T(8,128)} %param.7) | copy-start | bytes 393220
  0.7 18.8 %copy-start.3 = (f32[8,32,128]{2,1,0:T(8,128)S(1)}, f32[8,32,128]{2,1,0:T(8,128)}, u32[]{:S(2)}) copy-start(f32[8,32,128]{2,1,0:T(8,128)} %param.9) | copy-start | bytes 393220
  1.8 5.8 %collective-permute-start = (f32[3,4,32,128]{3,2,1,0:T(8,128)S(1)}, f32[3,4,32,128]{3,2,1,0:T(8,128)S(1)}, u32[]{:S(2)}, u32[]{:S(2)}) collective-permute-start(f32[3,4,32,128]{3,2,1,0:T(8,128)S(1)} %get-tuple-element.13), channel_id=1, source_target_pairs={{0,8},{8,16},{16,24},{24,0},{1,9},{9,17},{17,25},{25,1},{2,10},{10... | collective-permute-start | bytes 589832 | tf_op jit(solution)/shard_map/ppermute | solution.py:19
  2.4 7.2 %collective-permute-start.1 = (f32[3,4,32,128]{3,2,1,0:T(8,128)S(1)}, f32[3,4,32,128]{3,2,1,0:T(8,128)S(1)}, u32[]{:S(2)}, u32[]{:S(2)}) collective-permute-start(f32[3,4,32,128]{3,2,1,0:T(8,128)S(1)} %get-tuple-element.14), channel_id=1, source_target_pairs={{8,0},{16,8},{24,16},{0,24},{9,1},{17,9},{25,17},{1,25},{10,2},{18... | collective-permute-start | bytes 589832 | tf_op jit(solution)/shard_map/ppermute | solution.py:22
  10.5 7.5 %collective-permute-start.2 = (f32[3,16,4,128]{3,2,1,0:T(4,128)S(1)}, f32[3,16,4,128]{3,2,1,0:T(4,128)S(1)}, u32[]{:S(2)}, u32[]{:S(2)}) collective-permute-start(f32[3,16,4,128]{3,2,1,0:T(4,128)S(1)} %get-tuple-element.11), channel_id=1, source_target_pairs={{0,2},{2,4},{4,6},{6,0},{1,3},{3,5},{5,7},{7,1},{8,10},{10,12},{12... | collective-permute-start | bytes 294920 | tf_op jit(solution)/shard_map/ppermute | solution.py:19
  12.1 7.3 %collective-permute-start.3 = (f32[3,16,4,128]{3,2,1,0:T(4,128)S(1)}, f32[3,16,4,128]{3,2,1,0:T(4,128)S(1)}, u32[]{:S(2)}, u32[]{:S(2)}) collective-permute-start(f32[3,16,4,128]{3,2,1,0:T(4,128)S(1)} %get-tuple-element.12), channel_id=1, source_target_pairs={{2,0},{4,2},{6,4},{0,6},{3,1},{5,3},{7,5},{1,7},{10,8},{12,10},{14... | collective-permute-start | bytes 294920 | tf_op jit(solution)/shard_map/ppermute | solution.py:22
  19.9 2.9 %copy-start.5 = (f32[9,9]{1,0:T(8,128)S(1)}, f32[9,9]{1,0:T(8,128)}, u32[]{:S(2)}) copy-start(f32[9,9]{1,0:T(8,128)} %constant.17.clone) | copy-start | bytes 976
  20.3 5.4 %collective-permute-start.4 = (f32[3,16,40,4]{2,1,3,0:T(8,128)S(1)}, f32[3,16,40,4]{2,1,3,0:T(8,128)S(1)}, u32[]{:S(2)}, u32[]{:S(2)}) collective-permute-start(f32[3,16,40,4]{2,1,3,0:T(8,128)S(1)} %copy.18), channel_id=1, source_target_pairs={{0,1},{1,0},{2,3},{3,2},{4,5},{5,4},{6,7},{7,6},{8,9},{9,8},{10,11... | collective-permute-start | bytes 92168 | tf_op jit(solution)/shard_map/ppermute | solution.py:19
  22.2 4.9 %collective-permute-start.5 = (f32[3,16,40,4]{2,1,3,0:T(8,128)S(1)}, f32[3,16,40,4]{2,1,3,0:T(8,128)S(1)}, u32[]{:S(2)}, u32[]{:S(2)}) collective-permute-start(f32[3,16,40,4]{2,1,3,0:T(8,128)S(1)} %copy.19), channel_id=1, source_target_pairs={{1,0},{0,1},{3,2},{2,3},{5,4},{4,5},{7,6},{6,7},{9,8},{8,9},{11,10... | collective-permute-start | bytes 92168 | tf_op jit(solution)/shard_map/ppermute | solution.py:22
  104.5 5.1 %copy-start.4 = (bf16[16,8,32,128]{3,2,1,0:T(8,128)(2,1)S(1)}, bf16[16,8,32,128]{3,2,1,0:T(8,128)(2,1)}, u32[]{:S(2)}) copy-start(bf16[16,8,32,128]{3,2,1,0:T(8,128)(2,1)} %param.10) | copy-start | bytes 3145732
where the time goes:
time: 111 us
  blocking collectives  40 us (36%)
  matrix products  19.1 us (17%)
  waiting for transfers between devices  14 us (13%)
  between operations  11.8 us (11%)
  other arithmetic  10.2 us (9%)
  starting transfers between devices  8.58 us (8%)
  local copies, waits for them, and re-layouts  7.23 us (7%)
    psum x1, blocking collectives, body(): lax.psum(jnp.concatenate([gram_block, projections], 0), ('gx', 'gy', 'gz'))  40 us
    ppermute x3, waiting for transfers between devices, extended(): lax.ppermute(lax.slice_in_dim(block, block.shape[dim] - width, None, axis...  9.69 us
    ppermute x3, starting transfers between devices, extended(): lax.ppermute(lax.slice_in_dim(block, 0, width, axis=dim), axis, backward)  4.85 us
    ppermute x3, waiting for transfers between devices, extended(): lax.ppermute(lax.slice_in_dim(block, 0, width, axis=dim), axis, backward)  4.3 us
    another operation x2, local copies, waits for them, and re-layouts, body(): basis = jnp.stack(search_basis + residue_basis)  3.93 us
    sub x3, other arithmetic, chebyshev_next(): return 2.0 * scaled - earlier  3.83 us
    dot_general x5, matrix products, coordinates(): jnp.dot(gram_block, residue, precision=precise)  3.78 us
    ppermute x3, starting transfers between devices, extended(): lax.ppermute(lax.slice_in_dim(block, block.shape[dim] - width, None, axis...  3.73 us
  transfers between devices with their start and end apart: 6, of which 6 were waited for; matrix products, arithmetic and copies ran while one was open for 1% of the time, Pallas kernels for 0%

commit v1 on v0

--- a/solution.py
+++ b/solution.py
@@ -122,7 +122,9 @@
     projections = lax.dot_general(
         images, rounded, (((1,), (1,)), ((), ())), preferred_element_type=jnp.float32
     )
-    totals = lax.psum(jnp.concatenate([gram_block, projections], 0), ("gx", "gy", "gz"))
+    totals = jnp.concatenate([gram_block, projections], 0)
+    for ii in (("gy", "gz"), "gx"):
+        totals = jax.lax.psum(totals, axis_name=ii)
     update, residue, search, weights = coordinates(totals, coupling_inverse)
     shape = residual.shape
     solution_delta = jnp.dot(update, basis_flat, precision=precise).reshape(shape)

time: 111 us -> 97.5 us (0.88)
  blocking collectives: 40 us -> 26.1 us
    psum x1 -> x2, blocking collectives: 40 us -> 26.1 us  [body(): totals = jax.lax.psum(totals, axis_name=ii)]
where the time goes in v1:
time: 97.5 us; the launch traced here: 97.1 us
  blocking collectives  26.1 us (27%)
  matrix products  19.1 us (20%)
  waiting for transfers between devices  14 us (14%)
  between operations  11.8 us (12%)
  other arithmetic  10.2 us (10%)
  starting transfers between devices  8.58 us (9%)
  local copies, waits for them, and re-layouts  7.23 us (7%)
    psum x2, blocking collectives, body(): totals = jax.lax.psum(totals, axis_name=ii)  26.1 us
    ppermute x3, waiting for transfers between devices, extended(): lax.ppermute(lax.slice_in_dim(block, block.shape[dim] - width, None, axis...  9.69 us
    ppermute x3, starting transfers between devices, extended(): lax.ppermute(lax.slice_in_dim(block, 0, width, axis=dim), axis, backward)  4.85 us
    ppermute x3, waiting for transfers between devices, extended(): lax.ppermute(lax.slice_in_dim(block, 0, width, axis=dim), axis, backward)  4.3 us
    another operation x2, local copies, waits for them, and re-layouts, body(): basis = jnp.stack(search_basis + residue_basis)  3.93 us
    sub x3, other arithmetic, chebyshev_next(): return 2.0 * scaled - earlier  3.83 us
    dot_general x5, matrix products, coordinates(): jnp.dot(gram_block, residue, precision=precise)  3.78 us
    ppermute x3, starting transfers between devices, extended(): lax.ppermute(lax.slice_in_dim(block, block.shape[dim] - width, None, axis...  3.73 us
  transfers between devices with their start and end apart: 6, of which 6 were waited for; matrix products, arithmetic and copies ran while one was open for 1% of the time, Pallas kernels for 0%

profile of v1, /device:TPU:0, one launch (start us, length us, event | category | flops | bytes accessed | tf_op | source)
XLA Modules:
  0.0 97.1 jit_solution(14824524025075204334)
XLA Ops:
  0.7 1.1 %pad_maximum_fusion.2 = f32[3,8,32,128]{3,2,1,0:T(8,128)S(1)} fusion(f32[1,8,32,128]{3,2,1,0:T(8,128)} %bitcast.257, f32[1,8,32,128]{3,2,1,0:T(8,128)} %bitcast.251, f32[1,8,32,128]{3,2,1,0:T(8,128)} %bitcast.245), kind=kLoop, calls=%fused_computation.81 | loop fusion | flops 196608 | bytes 786432 | tf_op jit(solution)/shard_map/stack | solution.py:94
  1.8 0.5 collective-permute-start
  2.4 2.0 %collective-permute-start.1 = (f32[3,4,32,128]{3,2,1,0:T(8,128)S(1)}, f32[3,4,32,128]{3,2,1,0:T(8,128)S(1)}, u32[]{:S(2)}, u32[]{:S(2)}) collective-permute-start(f32[3,4,32,128]{3,2,1,0:T(8,128)S(1)} %get-tuple-element.14), channel_id=1, source_target_pairs={{8,0},{16,8},{24,16},{0,24},{9,1},{17,9},{25,17},{1,25},{10,2},{18... | collective-permute-start | bytes 589832 | tf_op jit(solution)/shard_map/ppermute | solution.py:22
  4.4 3.3 %collective-permute-done = f32[3,4,32,128]{3,2,1,0:T(8,128)S(1)} collective-permute-done((f32[3,4,32,128]{3,2,1,0:T(8,128)S(1)}, f32[3,4,32,128]{3,2,1,0:T(8,128)S(1)}, u32[]{:S(2)}, u32[]{:S(2)}) %collective-permute-start) | collective-permute-done | bytes 196640 | tf_op jit(solution)/shard_map/ppermute | solution.py:19
  7.7 1.9 %collective-permute-done.1 = f32[3,4,32,128]{3,2,1,0:T(8,128)S(1)} collective-permute-done((f32[3,4,32,128]{3,2,1,0:T(8,128)S(1)}, f32[3,4,32,128]{3,2,1,0:T(8,128)S(1)}, u32[]{:S(2)}, u32[]{:S(2)}) %collective-permute-start.1) | collective-permute-done | bytes 196640 | tf_op jit(solution)/shard_map/ppermute | solution.py:22
  9.6 0.9 pad_maximum_fusion.7
  10.5 1.6 %collective-permute-start.2 = (f32[3,16,4,128]{3,2,1,0:T(4,128)S(1)}, f32[3,16,4,128]{3,2,1,0:T(4,128)S(1)}, u32[]{:S(2)}, u32[]{:S(2)}) collective-permute-start(f32[3,16,4,128]{3,2,1,0:T(4,128)S(1)} %get-tuple-element.11), channel_id=1, source_target_pairs={{0,2},{2,4},{4,6},{6,0},{1,3},{3,5},{5,7},{7,1},{8,10},{10,12},{12... | collective-permute-start | bytes 294920 | tf_op jit(solution)/shard_map/ppermute | solution.py:19
  12.1 2.2 %collective-permute-start.3 = (f32[3,16,4,128]{3,2,1,0:T(4,128)S(1)}, f32[3,16,4,128]{3,2,1,0:T(4,128)S(1)}, u32[]{:S(2)}, u32[]{:S(2)}) collective-permute-start(f32[3,16,4,128]{3,2,1,0:T(4,128)S(1)} %get-tuple-element.12), channel_id=1, source_target_pairs={{2,0},{4,2},{6,4},{0,6},{3,1},{5,3},{7,5},{1,7},{10,8},{12,10},{14... | collective-permute-start | bytes 294920 | tf_op jit(solution)/shard_map/ppermute | solution.py:22
  14.4 3.7 %collective-permute-done.2 = f32[3,16,4,128]{3,2,1,0:T(4,128)S(1)} collective-permute-done((f32[3,16,4,128]{3,2,1,0:T(4,128)S(1)}, f32[3,16,4,128]{3,2,1,0:T(4,128)S(1)}, u32[]{:S(2)}, u32[]{:S(2)}) %collective-permute-start.2) | collective-permute-done | bytes 98336 | tf_op jit(solution)/shard_map/ppermute | solution.py:19
  18.0 1.4 %collective-permute-done.3 = f32[3,16,4,128]{3,2,1,0:T(4,128)S(1)} collective-permute-done((f32[3,16,4,128]{3,2,1,0:T(4,128)S(1)}, f32[3,16,4,128]{3,2,1,0:T(4,128)S(1)}, u32[]{:S(2)}, u32[]{:S(2)}) %collective-permute-start.3) | collective-permute-done | bytes 98336 | tf_op jit(solution)/shard_map/ppermute | solution.py:22
  19.4 0.1 pad_maximum_fusion.1
  19.6 0.3 fusion.105
  19.9 0.4 copy.18
  20.3 1.6 %collective-permute-start.4 = (f32[3,16,40,4]{2,1,3,0:T(8,128)S(1)}, f32[3,16,40,4]{2,1,3,0:T(8,128)S(1)}, u32[]{:S(2)}, u32[]{:S(2)}) collective-permute-start(f32[3,16,40,4]{2,1,3,0:T(8,128)S(1)} %copy.18), channel_id=1, source_target_pairs={{0,1},{1,0},{2,3},{3,2},{4,5},{5,4},{6,7},{7,6},{8,9},{9,8},{10,11... | collective-permute-start | bytes 92168 | tf_op jit(solution)/shard_map/ppermute | solution.py:19
  21.8 0.4 copy.19
  22.2 0.6 collective-permute-start.5
  22.8 0.1 fusion.55
  22.9 2.8 %collective-permute-done.4 = f32[3,16,40,4]{2,1,3,0:T(8,128)S(1)} collective-permute-done((f32[3,16,40,4]{2,1,3,0:T(8,128)S(1)}, f32[3,16,40,4]{2,1,3,0:T(8,128)S(1)}, u32[]{:S(2)}, u32[]{:S(2)}) %collective-permute-start.4) | collective-permute-done | bytes 30752 | tf_op jit(solution)/shard_map/ppermute | solution.py:19
  25.7 0.4 copy.20
  26.1 1.0 collective-permute-done.5
  27.1 0.4 copy.21
  27.5 1.1 %pad_maximum_fusion = f32[3,16,40,136]{3,2,1,0:T(8,128)S(1)} fusion(f32[3,16,40,4]{3,2,1,0:T(8,128)S(1)} %copy.21, f32[3,16,4,128]{3,2,1,0:T(4,128)S(1)} %collective-permute-done.3, f32[3,4,32,128]{3,2,1,0:T(8,128)S(1)} %collective-permute-done.1, f32[1,8,32,128]{3,2,1,0:T(8,128)S(1)} %bitcast.260, f32[1,8,32,128]{3,2,1,0:T(8,128)S(1)} %bitcast.254, ...), kind=kLoop, calls=%fused_computation.4 | loop fusion | flops 2088960 | bytes 2088960 | tf_op jit(solution)/shard_map/concatenate | solution.py:23
  28.6 0.2 slice_add_fusion.15
  28.8 0.2 slice_add_fusion.16
  29.0 0.2 slice_add_fusion.17
  29.2 1.9 %fusion.6 = f32[2,14,38,134]{3,2,1,0:T(8,128)S(1)} fusion(f32[3,16,40,136]{3,2,1,0:T(8,128)S(1)} %pad_maximum_fusion, f32[14,38,134]{2,1,0:T(8,128)S(1)} %slice_add_fusion.15), kind=kLoop, calls=%fused_computation.8 | loop fusion | flops 1425760 | bytes 4847584 | tf_op jit(solution)/shard_map/div | solution.py:43
  31.1 1.9 %slice_subtract_fusion = f32[2,12,36,132]{3,2,1,0:T(8,128)S(1)} fusion(f32[3,16,40,136]{3,2,1,0:T(8,128)S(1)} %pad_maximum_fusion, f32[2,14,38,134]{3,2,1,0:T(8,128)S(1)} %fusion.6, f32[12,36,132]{2,1,0:T(8,128)S(1)} %slice_add_fusion.16), kind=kLoop, calls=%fused_computation.43 | loop fusion | flops 1254528 | bytes 4333824 | tf_op jit(solution)/shard_map/sub | solution.py:46
  33.0 1.6 %slice_subtract_fusion.1 = f32[2,10,34,130]{3,2,1,0:T(8,128)S(1)} fusion(f32[2,14,38,134]{3,2,1,0:T(8,128)S(1)} %fusion.6, f32[2,12,36,132]{3,2,1,0:T(8,128)S(1)} %slice_subtract_fusion, f32[10,34,130]{2,1,0:T(8,128)S(1)} %slice_add_fusion.17), kind=kLoop, calls=%fused_computation.53 | loop fusion | flops 972400 | bytes 3359200 | tf_op jit(solution)/shard_map/sub | solution.py:46
  34.6 0.3 slice_subtract_fusion.2
  35.1 0.1 slice_bitcast_fusion.1
  35.1 0.1 slice.279
  35.3 0.1 slice.294
  35.4 0.1 slice.268
  35.5 0.1 slice.292
  35.6 0.1 slice.290
  35.7 0.1 slice.257
  35.8 2.1 %stack.65 = f32[9,8,32,128]{3,0,2,1:T(8,128)S(1)} concatenate(f32[1,8,32,128]{3,0,2,1:T(1,128)S(1)} %bitcast.249, f32[1,8,32,128]{3,0,2,1:T(1,128)S(1)} %bitcast.273, f32[1,8,32,128]{3,0,2,1:T(1,128)S(1)} %bitcast.267, f32[1,8,32,128]{3,0,2,1:T(1,128)S(1)} %bitcast.263, f32[1,8,32,128]{3,0,2,1:T(1,128)S(1)} %bitcast.261, f32[1,8,32,128]{3,0,2,1:T(1,128)S(1)} %bitcast.255, ...), dimensions={0} | concatenate | bytes 2359296 | tf_op jit(solution)/shard_map/stack | solution.py:111
  37.8 2.9 %convolution_bitcast_fusion.1 = f32[9,9]{0,1:T(8,128)S(1)} fusion(f32[9,8,32,128]{3,0,2,1:T(8,128)S(1)} %stack.65), kind=kOutput, calls=%fused_computation.14 | convolution fusion | flops 31850496 | bytes 1179972 | tf_op jit(solution)/shard_map/dot_general | solution.py:113
  40.7 1.9 %stack.75 = f32[9,32768]{1,0:T(8,128)S(1)} concatenate(f32[1,32768]{1,0:T(1,128)S(1)} %bitcast.250, f32[1,32768]{1,0:T(1,128)S(1)} %bitcast.274, f32[1,32768]{1,0:T(1,128)S(1)} %bitcast.268, f32[1,32768]{1,0:T(1,128)S(1)} %bitcast.264, f32[1,32768]{1,0:T(1,128)S(1)} %bitcast.262, f32[1,32768]{1,0:T(1,128)S(1)} %bitcast.256, f32[1,32768]{1,0:T(1,128)S(1)} %bitcast.272, ...), dimensions={0} | concatenate | bytes 2359296 | tf_op jit(solution)/shard_map/stack | solution.py:111
  42.6 2.0 %convolution_bitcast_fusion = f32[16,9]{0,1:T(8,128)S(1)} fusion(bf16[2,8,256,128]{3,2,1,0:T(8,128)(2,1)} %bitcast.275, f32[9,32768]{1,0:T(8,128)S(1)} %stack.75), kind=kOutput, calls=%fused_computation.13 | convolution fusion | flops 9732096 | bytes 2228800 | tf_op jit(solution)/shard_map/dot_general | solution.py:122
  44.6 0.1 pad_maximum_fusion.8
  44.7 20.4 %psum.14 = f32[25,9]{0,1:T(8,128)S(1)} all-reduce(f32[25,9]{0,1:T(8,128)S(1)} %pad_maximum_fusion.8), channel_id=1, replica_groups=mesh['gx'=4,'gy'=4,'gz'=2] {'gy','gz'}, use_global_device_ids=true, to_apply=%region_0.0 | all-reduce | flops 225 | bytes 1800 | tf_op jit(solution)/shard_map/psum | solution.py:127
  65.1 5.8 %psum.15 = f32[25,9]{0,1:T(8,128)S(1)} all-reduce(f32[25,9]{0,1:T(8,128)S(1)} %psum.14), channel_id=1, replica_groups=mesh['gx'=4,'gy'=4,'gz'=2] {'gx'}, use_global_device_ids=true, to_apply=%region_1.0 | all-reduce | flops 225 | bytes 1800 | tf_op jit(solution)/shard_map/psum | solution.py:127
  70.9 0.7 fusion.31
  71.6 0.7 fusion.30
  73.7 0.7 fusion.32
  75.8 0.1 fusion.89
  75.9 0.8 fusion.33
  78.0 0.7 fusion.34
  80.1 0.1 fusion.87
  80.2 0.8 fusion.35
  82.3 0.8 fusion.36
  84.5 0.1 fusion.85
  84.7 0.8 fusion.37
  86.8 0.2 convolution_bitcast_fusion.3
  87.0 0.7 fusion.38
  87.8 0.4 copy.55
  88.2 0.1 slice.297
  88.3 2.4 %fusion = f32[1,8,32,128]{3,0,2,1:T(1,128)} fusion(f32[8,32,128,9]{2,1,0,3:T(8,128)S(1)} %bitcast.242, f32[9]{0:T(128)S(1)} %fusion.67), kind=kOutput, calls=%fused_computation | convolution fusion | flops 3538944 | bytes 1310756 | tf_op jit(solution)/shard_map/dot_general | solution.py:131
  90.7 2.4 %fusion.2 = f32[1,8,32,128]{3,0,2,1:T(1,128)} fusion(f32[8,32,128,9]{2,1,0,3:T(8,128)S(1)} %bitcast.243, f32[9]{0:T(128)S(1)} %multiply_add_fusion, f32[9]{0:T(128)S(1)} %multiply_add_fusion.1, f32[9]{0:T(128)S(1)} %select_add_fusion, f32[]{:T(128)S(6)} %div.44, f32[]{:T(128)S(6)} %div.42, f32[]{:T(128)S(6)} %div.40, f32[]{:T(128)S(6)} %div.38), kind=kOutput, calls=%fused_computation.2 | convolution fusion | flops 3539016 | bytes 1310844 | tf_op jit(solution)/shard_map/dot_general | solution.py:130
  94.5 1.1 %fusion.62 = f32[1,32768]{1,0:T(1,128)S(1)} fusion(f32[9,32768]{1,0:T(8,128)S(1)} %stack.75, f32[9]{0:T(128)S(1)} %fusion.67, f32[9]{0:T(128)S(1)} %multiply_add_fusion, f32[]{:T(128)S(6)} %div.45), kind=kOutput, calls=%fused_computation.119 | convolution fusion | flops 3538962 | bytes 1310796 | tf_op jit(solution)/shard_map/dot_general | solution.py:135
  95.6 0.1 fusion.15
  95.7 0.7 fusion.18
  96.4 0.7 sub.63
  (22 shorter events, 0.3 us)
Async XLA Ops:
  0.6 95.0 %copy-start = (f32[16,16]{1,0:T(8,128)S(1)}, f32[16,16]{1,0:T(8,128)}, u32[]{:S(2)}) copy-start(f32[16,16]{1,0:T(8,128)} %param.12) | copy-start | bytes 3076
  0.6 18.8 %copy-start.1 = (f32[8,32,128]{2,1,0:T(8,128)S(1)}, f32[8,32,128]{2,1,0:T(8,128)}, u32[]{:S(2)}) copy-start(f32[8,32,128]{2,1,0:T(8,128)} %param.8) | copy-start | bytes 393220
  0.7 18.8 %copy-start.2 = (f32[8,32,128]{2,1,0:T(8,128)S(1)}, f32[8,32,128]{2,1,0:T(8,128)}, u32[]{:S(2)}) copy-start(f32[8,32,128]{2,1,0:T(8,128)} %param.7) | copy-start | bytes 393220
  0.7 18.8 %copy-start.3 = (f32[8,32,128]{2,1,0:T(8,128)S(1)}, f32[8,32,128]{2,1,0:T(8,128)}, u32[]{:S(2)}) copy-start(f32[8,32,128]{2,1,0:T(8,128)} %param.9) | copy-start | bytes 393220
  1.8 5.8 %collective-permute-start = (f32[3,4,32,128]{3,2,1,0:T(8,128)S(1)}, f32[3,4,32,128]{3,2,1,0:T(8,128)S(1)}, u32[]{:S(2)}, u32[]{:S(2)}) collective-permute-start(f32[3,4,32,128]{3,2,1,0:T(8,128)S(1)} %get-tuple-element.13), channel_id=1, source_target_pairs={{0,8},{8,16},{16,24},{24,0},{1,9},{9,17},{17,25},{25,1},{2,10},{10... | collective-permute-start | bytes 589832 | tf_op jit(solution)/shard_map/ppermute | solution.py:19
  2.4 7.2 %collective-permute-start.1 = (f32[3,4,32,128]{3,2,1,0:T(8,128)S(1)}, f32[3,4,32,128]{3,2,1,0:T(8,128)S(1)}, u32[]{:S(2)}, u32[]{:S(2)}) collective-permute-start(f32[3,4,32,128]{3,2,1,0:T(8,128)S(1)} %get-tuple-element.14), channel_id=1, source_target_pairs={{8,0},{16,8},{24,16},{0,24},{9,1},{17,9},{25,17},{1,25},{10,2},{18... | collective-permute-start | bytes 589832 | tf_op jit(solution)/shard_map/ppermute | solution.py:22
  10.5 7.5 %collective-permute-start.2 = (f32[3,16,4,128]{3,2,1,0:T(4,128)S(1)}, f32[3,16,4,128]{3,2,1,0:T(4,128)S(1)}, u32[]{:S(2)}, u32[]{:S(2)}) collective-permute-start(f32[3,16,4,128]{3,2,1,0:T(4,128)S(1)} %get-tuple-element.11), channel_id=1, source_target_pairs={{0,2},{2,4},{4,6},{6,0},{1,3},{3,5},{5,7},{7,1},{8,10},{10,12},{12... | collective-permute-start | bytes 294920 | tf_op jit(solution)/shard_map/ppermute | solution.py:19
  12.1 7.3 %collective-permute-start.3 = (f32[3,16,4,128]{3,2,1,0:T(4,128)S(1)}, f32[3,16,4,128]{3,2,1,0:T(4,128)S(1)}, u32[]{:S(2)}, u32[]{:S(2)}) collective-permute-start(f32[3,16,4,128]{3,2,1,0:T(4,128)S(1)} %get-tuple-element.12), channel_id=1, source_target_pairs={{2,0},{4,2},{6,4},{0,6},{3,1},{5,3},{7,5},{1,7},{10,8},{12,10},{14... | collective-permute-start | bytes 294920 | tf_op jit(solution)/shard_map/ppermute | solution.py:22
  19.9 2.9 %copy-start.5 = (f32[9,9]{1,0:T(8,128)S(1)}, f32[9,9]{1,0:T(8,128)}, u32[]{:S(2)}) copy-start(f32[9,9]{1,0:T(8,128)} %constant.17.clone) | copy-start | bytes 976
  20.3 5.4 %collective-permute-start.4 = (f32[3,16,40,4]{2,1,3,0:T(8,128)S(1)}, f32[3,16,40,4]{2,1,3,0:T(8,128)S(1)}, u32[]{:S(2)}, u32[]{:S(2)}) collective-permute-start(f32[3,16,40,4]{2,1,3,0:T(8,128)S(1)} %copy.18), channel_id=1, source_target_pairs={{0,1},{1,0},{2,3},{3,2},{4,5},{5,4},{6,7},{7,6},{8,9},{9,8},{10,11... | collective-permute-start | bytes 92168 | tf_op jit(solution)/shard_map/ppermute | solution.py:19
  22.2 4.9 %collective-permute-start.5 = (f32[3,16,40,4]{2,1,3,0:T(8,128)S(1)}, f32[3,16,40,4]{2,1,3,0:T(8,128)S(1)}, u32[]{:S(2)}, u32[]{:S(2)}) collective-permute-start(f32[3,16,40,4]{2,1,3,0:T(8,128)S(1)} %copy.19), channel_id=1, source_target_pairs={{1,0},{0,1},{3,2},{2,3},{5,4},{4,5},{7,6},{6,7},{9,8},{8,9},{11,10... | collective-permute-start | bytes 92168 | tf_op jit(solution)/shard_map/ppermute | solution.py:22
  90.7 5.1 %copy-start.4 = (bf16[16,8,32,128]{3,2,1,0:T(8,128)(2,1)S(1)}, bf16[16,8,32,128]{3,2,1,0:T(8,128)(2,1)}, u32[]{:S(2)}) copy-start(bf16[16,8,32,128]{3,2,1,0:T(8,128)(2,1)} %param.10) | copy-start | bytes 3145732
